TPU v7x, 32 devices: a whole 2x2x4 slice. The times are simulated.
32 devices in a mesh: tm: 8 (over y, x, core), space: 4 (over z).
Axes of the slice: x: 2, y: 2, z: 4, core: 2. Of those that a mesh axis runs over, the one named last changes fastest.
Arguments:
- previous_end: float32 [8, 16, 256, 256], P('tm', 'space'), may hold values from -6 to 6
- source: float32 [8, 16, 256, 256], P('tm', 'space'), may hold values from -4 to 4
- rate: float32 [16, 256, 256], P('space'), may hold values from 0.05 to 0.8
Outputs:
- fine_nodes: float32 [8, 2, 16, 256, 256], P('tm', None, 'space')
All inputs are finite; a program needn't handle non-finite values.
Results may differ from a plain program's by a relative error of at most 0.00026.
Values sent between devices are 32-bit elements; how exact they have to be, the bound alone decides.
A program may use at most 128 MiB of HBM per device.

v0:
```python
import jax
import jax.numpy as jnp
from jax import lax
from jax.sharding import PartitionSpec as P

diffusion = 0.1
speed_z = 0.4
speed_x = 0.3
speed_y = 0.2
weights_one = (5.0 / 24.0, 1.0 / 3.0, -1.0 / 24.0)
weights_two = (-1.0 / 24.0, 1.0 / 3.0, 5.0 / 24.0)


def broadcast(array, axis, root):
    mine = lax.axis_index(axis) == root
    return lax.psum(jnp.where(mine, array, jnp.zeros_like(array)), axis)


def padded_2(array, sides, width):
    for axis, dim in sides:
        size, length = (lax.axis_size(axis), array.shape[dim])
        up = [(i, (i + 1) % size) for i in range(size - 1)]
        down = [(j, i) for i, j in up]
        last = lax.slice_in_dim(array, length - width, length, axis=dim)
        first = lax.slice_in_dim(array, 0, width, axis=dim)
        before = lax.ppermute(last, axis, up)
        after = lax.ppermute(first, axis, down)
        array = jnp.concatenate([before, array, after], axis=dim)
    return array


def shifted(value, axis, steps):
    count = lax.axis_size(axis)
    first, last = (max(0, -steps), min(count, count - steps))
    return lax.ppermute(value, axis, [(source, source + steps) for source in range(first, last)])


def tendency(padded, rate_field, source_term, spacing):
    middle = padded[..., 1:-1, :, :]
    upper_z = padded[..., 2:, :, :]
    lower_z = padded[..., :-2, :, :]
    plus_x = jnp.roll(middle, -1, axis=-2)
    minus_x = jnp.roll(middle, 1, axis=-2)
    plus_y = jnp.roll(middle, -1, axis=-1)
    minus_y = jnp.roll(middle, 1, axis=-1)
    laplacian = (upper_z + lower_z + plus_x + minus_x + plus_y + minus_y - 6.0 * middle) / (
        spacing * spacing
    )
    transport = (
        speed_z * (upper_z - lower_z) + speed_x * (plus_x - minus_x) + speed_y * (plus_y - minus_y)
    ) / (2.0 * spacing)
    return (
        diffusion * laplacian
        - transport
        + rate_field * middle / (1.0 + middle * middle)
        + source_term
    )


def pair_table(count):
    fine_index = jnp.arange(count, dtype=jnp.int32)[:, None]
    coarse_index = jnp.arange(count // 2, dtype=jnp.int32)[None, :]
    return (fine_index // 2 == coarse_index).astype(jnp.float32)


def restrict(field):
    count_z, count_x, count_y = field.shape[-3:]
    paired = field.reshape(field.shape[:-3] + (count_z // 2, 2, count_x, count_y))
    summed_z = paired[..., 0, :, :] + paired[..., 1, :, :]
    summed_y = jnp.einsum(
        "...xy,yb->...xb", summed_z, pair_table(count_y), precision=lax.Precision.HIGHEST
    )
    summed_x = jnp.einsum(
        "...xb,xa->...ab", summed_y, pair_table(count_x), precision=lax.Precision.HIGHEST
    )
    return 0.125 * summed_x


def inject(coarse):
    count_x, count_y = coarse.shape[-2:]
    along_y = jnp.einsum(
        "...ab,yb->...ay", coarse, pair_table(2 * count_y), precision=lax.Precision.HIGHEST
    )
    along_x = jnp.einsum(
        "...ay,xa->...xy", along_y, pair_table(2 * count_x), precision=lax.Precision.HIGHEST
    )
    return jnp.repeat(along_x, 2, axis=-3)


def pick(stacked, index):
    return lax.dynamic_index_in_dim(stacked, index, 0, keepdims=False)


def broadcast_seed(warm):
    return broadcast(warm, "tm", lax.axis_size("tm") - 1)


def widen(stacked):
    return padded_2(stacked, (("space", 1),), 1)


def coarse_deep(start, rate_c, source_c, rate_wide, source_wide):
    padded = padded_2(start, (("space", 0),), 2)
    first_wide = padded[1:-1] + 0.5 * tendency(padded, rate_wide, source_wide, 2.0)
    count_z = start.shape[0]
    global_z = lax.axis_index("space") * count_z - 1 + jnp.arange(count_z + 2, dtype=jnp.int32)
    inside = (global_z >= 0) & (global_z < count_z * lax.axis_size("space"))
    first_wide = jnp.where(inside[:, None, None], first_wide, 0.0)
    second = first_wide[1:-1] + 0.5 * tendency(first_wide, rate_c, source_c, 2.0)
    return (first_wide[1:-1], second)


def coarse_pair(start, stacked, wide, index):
    return coarse_deep(start, stacked[0], pick(stacked, index), wide[0], pick(wide, index))


def shards(previous_end, source, rate):
    warm = previous_end[0]
    own_source = source[0]
    rank = lax.axis_index("tm")
    turns = lax.axis_size("tm") - 1
    rate_c = restrict(rate)
    source_c = restrict(own_source)
    stacked = jnp.stack([rate_c, source_c])
    wide = widen(stacked)
    restart = broadcast_seed(warm)
    restart_c = restrict(restart)

    def turn(step, value):
        first, second = coarse_pair(value, stacked, wide, 1)
        moved = shifted(second, "tm", 1)
        return jnp.where(rank == 0, restart_c, moved)

    start = lax.fori_loop(0, turns, turn, restart_c)
    first, second = coarse_pair(start, stacked, wide, 1)
    warm_c = restrict(warm)
    guess = jnp.stack(
        [
            restart + inject(start - restart_c),
            warm + inject(first - warm_c),
            warm + inject(second - warm_c),
        ]
    )
    padded = padded_2(guess, (("space", 1),), 1)
    images = tendency(padded, rate, own_source, 1.0)
    node_one = guess[0] + (
        weights_one[0] * images[0] + weights_one[1] * images[1] + weights_one[2] * images[2]
    )
    padded_one = padded_2(node_one, (("space", 0),), 1)
    again = tendency(padded_one, rate, own_source, 1.0)
    node_two = (
        node_one
        + 0.5 * (again - images[1])
        + (weights_two[0] * images[0] + weights_two[1] * images[1] + weights_two[2] * images[2])
    )
    return jnp.stack([node_one, node_two])[None]


def solution(mesh):
    placed = (P("tm", "space", None, None), P("tm", "space", None, None), P("space", None, None))
    return jax.shard_map(
        shards,
        mesh=mesh,
        in_specs=placed,
        out_specs=P("tm", None, "space", None, None),
        check_vma=False,
    )
```

profile of v0, /device:TPU:2, one launch (start us, length us, event | category | flops | bytes accessed | tf_op | source)
XLA Modules:
  0.0 267.3 jit_solution(10038256187280063621)
XLA Ops:
  6.5 1.7 fusion.18
  8.7 1.7 fusion.22
  10.7 3.5 %collective-permute-start.3 = (f32[2,1,128,128]{3,2,1,0:T(8,128)S(1)}, f32[2,1,128,128]{3,2,1,0:T(8,128)S(1)}, u32[]{:S(2)}, u32[]{:S(2)}) collective-permute-start(f32[2,1,128,128]{3,2,1,0:T(8,128)S(1)} %get-tuple-element.197), channel_id=1, source_target_pairs={{0,1},{1,2},{2,3},{4,5},{5,6},{6,7},{8,9},{9,10},{10,11},{12,13},{... | collective-permute-start | bytes 393224 | tf_op jit(solution)/shard_map/ppermute | solution.py:26
  14.2 1.3 collective-permute-start.4
  18.2 2.9 %collective-permute-done.4 = f32[2,1,128,128]{3,2,1,0:T(8,128)S(1)} collective-permute-done((f32[2,1,128,128]{3,2,1,0:T(8,128)S(1)}, f32[2,1,128,128]{3,2,1,0:T(8,128)S(1)}, u32[]{:S(2)}, u32[]{:S(2)}) %collective-permute-start.4) | collective-permute-done | bytes 131104 | tf_op jit(solution)/shard_map/ppermute | solution.py:27
  21.1 53.8 %all-reduce.2.cloned.1.call-done = f32[4,256,256]{2,1,0:T(8,128)} async-done(((f32[4,256,256]{2,1,0:T(8,128)}), f32[4,256,256]{2,1,0:T(8,128)}) %all-reduce.2.cloned.1.call-update) | async-done | bytes 1048592 | tf_op jit(solution)/shard_map/psum | solution.py:16
  74.9 1.6 fusion.26
  77.0 122.6 %while.13 = (s32[]{:T(128)}, f32[2,128,128]{2,1,0:T(8,128)S(1)}, pred[]{:T(512)}, f32[2,4,128,128]{3,2,1,0:T(8,128)S(1)}, f32[2,128,128]{2,1,0:T(8,128)S(1)}, /*...) while((s32[]{:T(128)}, f32[2,128,128]{2,1,0:T(8,128)S(1)}, ...), condition=%wide.region_2.3_spmd, body=%wide.region_1.2_spmd.sunk | while | flops 3047446 | bytes 10354974 | solution.py:134
  77.0 3.5 %collective-permute-start = (f32[2,128,128]{2,1,0:T(8,128)S(1)}, f32[2,128,128]{2,1,0:T(8,128)S(1)}, u32[]{:S(2)}, u32[]{:S(2)}) collective-permute-start(f32[2,128,128]{2,1,0:T(8,128)S(1)} %get-tuple-element.307), channel_id=1, source_target_pairs={{0,1},{1,2},{2,3},{4,5},{5,6},{6,7},{8,9},{9,10},{10,11},{12,13},{... | collective-permute-start | bytes 393224 | tf_op jit(solution)/shard_map/while/body/eval_jaxpr/ppermute | solution.py:26
  80.5 1.3 collective-permute-start.1
  81.8 1.2 collective-permute-done
  83.1 4.3 %collective-permute-done.1 = f32[2,128,128]{2,1,0:T(8,128)S(1)} collective-permute-done((f32[2,128,128]{2,1,0:T(8,128)S(1)}, f32[2,128,128]{2,1,0:T(8,128)S(1)}, u32[]{:S(2)}, u32[]{:S(2)}) %collective-permute-start.1) | collective-permute-done | bytes 131104 | tf_op jit(solution)/shard_map/while/body/eval_jaxpr/ppermute | solution.py:27
  88.6 1.9 collective-permute-start.2
  90.5 4.4 %collective-permute-done.2 = f32[2,128,128]{2,1,0:T(8,128)S(1)} collective-permute-done((f32[2,128,128]{2,1,0:T(8,128)S(1)}, f32[2,128,128]{2,1,0:T(8,128)S(1)}, u32[]{:S(2)}, u32[]{:S(2)}) %collective-permute-start.2) | collective-permute-done | bytes 131104 | tf_op jit(solution)/shard_map/while/body/eval_jaxpr/ppermute | solution.py:35
  94.9 3.4 %collective-permute-start = (f32[2,128,128]{2,1,0:T(8,128)S(1)}, f32[2,128,128]{2,1,0:T(8,128)S(1)}, u32[]{:S(2)}, u32[]{:S(2)}) collective-permute-start(f32[2,128,128]{2,1,0:T(8,128)S(1)} %get-tuple-element.307), channel_id=1, source_target_pairs={{0,1},{1,2},{2,3},{4,5},{5,6},{6,7},{8,9},{9,10},{10,11},{12,13},{... | collective-permute-start | bytes 393224 | tf_op jit(solution)/shard_map/while/body/eval_jaxpr/ppermute | solution.py:26
  98.3 1.3 collective-permute-start.1
  100.9 4.3 %collective-permute-done.1 = f32[2,128,128]{2,1,0:T(8,128)S(1)} collective-permute-done((f32[2,128,128]{2,1,0:T(8,128)S(1)}, f32[2,128,128]{2,1,0:T(8,128)S(1)}, u32[]{:S(2)}, u32[]{:S(2)}) %collective-permute-start.1) | collective-permute-done | bytes 131104 | tf_op jit(solution)/shard_map/while/body/eval_jaxpr/ppermute | solution.py:27
  106.4 1.9 collective-permute-start.2
  108.3 4.4 %collective-permute-done.2 = f32[2,128,128]{2,1,0:T(8,128)S(1)} collective-permute-done((f32[2,128,128]{2,1,0:T(8,128)S(1)}, f32[2,128,128]{2,1,0:T(8,128)S(1)}, u32[]{:S(2)}, u32[]{:S(2)}) %collective-permute-start.2) | collective-permute-done | bytes 131104 | tf_op jit(solution)/shard_map/while/body/eval_jaxpr/ppermute | solution.py:35
  112.7 3.4 %collective-permute-start = (f32[2,128,128]{2,1,0:T(8,128)S(1)}, f32[2,128,128]{2,1,0:T(8,128)S(1)}, u32[]{:S(2)}, u32[]{:S(2)}) collective-permute-start(f32[2,128,128]{2,1,0:T(8,128)S(1)} %get-tuple-element.307), channel_id=1, source_target_pairs={{0,1},{1,2},{2,3},{4,5},{5,6},{6,7},{8,9},{9,10},{10,11},{12,13},{... | collective-permute-start | bytes 393224 | tf_op jit(solution)/shard_map/while/body/eval_jaxpr/ppermute | solution.py:26
  116.1 1.3 collective-permute-start.1
  117.4 1.6 collective-permute-done
  119.1 4.1 %collective-permute-done.1 = f32[2,128,128]{2,1,0:T(8,128)S(1)} collective-permute-done((f32[2,128,128]{2,1,0:T(8,128)S(1)}, f32[2,128,128]{2,1,0:T(8,128)S(1)}, u32[]{:S(2)}, u32[]{:S(2)}) %collective-permute-start.1) | collective-permute-done | bytes 131104 | tf_op jit(solution)/shard_map/while/body/eval_jaxpr/ppermute | solution.py:27
  124.4 1.9 collective-permute-start.2
  126.3 4.4 %collective-permute-done.2 = f32[2,128,128]{2,1,0:T(8,128)S(1)} collective-permute-done((f32[2,128,128]{2,1,0:T(8,128)S(1)}, f32[2,128,128]{2,1,0:T(8,128)S(1)}, u32[]{:S(2)}, u32[]{:S(2)}) %collective-permute-start.2) | collective-permute-done | bytes 131104 | tf_op jit(solution)/shard_map/while/body/eval_jaxpr/ppermute | solution.py:35
  130.7 2.2 collective-permute-start
  132.9 1.3 collective-permute-start.1
  134.2 2.0 collective-permute-done
  136.3 4.1 %collective-permute-done.1 = f32[2,128,128]{2,1,0:T(8,128)S(1)} collective-permute-done((f32[2,128,128]{2,1,0:T(8,128)S(1)}, f32[2,128,128]{2,1,0:T(8,128)S(1)}, u32[]{:S(2)}, u32[]{:S(2)}) %collective-permute-start.1) | collective-permute-done | bytes 131104 | tf_op jit(solution)/shard_map/while/body/eval_jaxpr/ppermute | solution.py:27
  141.6 1.9 collective-permute-start.2
  143.5 4.4 %collective-permute-done.2 = f32[2,128,128]{2,1,0:T(8,128)S(1)} collective-permute-done((f32[2,128,128]{2,1,0:T(8,128)S(1)}, f32[2,128,128]{2,1,0:T(8,128)S(1)}, u32[]{:S(2)}, u32[]{:S(2)}) %collective-permute-start.2) | collective-permute-done | bytes 131104 | tf_op jit(solution)/shard_map/while/body/eval_jaxpr/ppermute | solution.py:35
  147.9 2.2 collective-permute-start
  150.1 1.3 collective-permute-start.1
  151.4 2.0 collective-permute-done
  153.5 4.1 %collective-permute-done.1 = f32[2,128,128]{2,1,0:T(8,128)S(1)} collective-permute-done((f32[2,128,128]{2,1,0:T(8,128)S(1)}, f32[2,128,128]{2,1,0:T(8,128)S(1)}, u32[]{:S(2)}, u32[]{:S(2)}) %collective-permute-start.1) | collective-permute-done | bytes 131104 | tf_op jit(solution)/shard_map/while/body/eval_jaxpr/ppermute | solution.py:27
  158.8 1.9 collective-permute-start.2
  160.7 4.4 %collective-permute-done.2 = f32[2,128,128]{2,1,0:T(8,128)S(1)} collective-permute-done((f32[2,128,128]{2,1,0:T(8,128)S(1)}, f32[2,128,128]{2,1,0:T(8,128)S(1)}, u32[]{:S(2)}, u32[]{:S(2)}) %collective-permute-start.2) | collective-permute-done | bytes 131104 | tf_op jit(solution)/shard_map/while/body/eval_jaxpr/ppermute | solution.py:35
  165.1 2.2 collective-permute-start
  167.3 1.3 collective-permute-start.1
  168.6 2.0 collective-permute-done
  170.7 4.1 %collective-permute-done.1 = f32[2,128,128]{2,1,0:T(8,128)S(1)} collective-permute-done((f32[2,128,128]{2,1,0:T(8,128)S(1)}, f32[2,128,128]{2,1,0:T(8,128)S(1)}, u32[]{:S(2)}, u32[]{:S(2)}) %collective-permute-start.1) | collective-permute-done | bytes 131104 | tf_op jit(solution)/shard_map/while/body/eval_jaxpr/ppermute | solution.py:27
  176.0 1.9 collective-permute-start.2
  177.9 4.4 %collective-permute-done.2 = f32[2,128,128]{2,1,0:T(8,128)S(1)} collective-permute-done((f32[2,128,128]{2,1,0:T(8,128)S(1)}, f32[2,128,128]{2,1,0:T(8,128)S(1)}, u32[]{:S(2)}, u32[]{:S(2)}) %collective-permute-start.2) | collective-permute-done | bytes 131104 | tf_op jit(solution)/shard_map/while/body/eval_jaxpr/ppermute | solution.py:35
  182.3 2.2 collective-permute-start
  184.5 1.3 collective-permute-start.1
  185.9 2.0 collective-permute-done
  188.0 4.1 %collective-permute-done.1 = f32[2,128,128]{2,1,0:T(8,128)S(1)} collective-permute-done((f32[2,128,128]{2,1,0:T(8,128)S(1)}, f32[2,128,128]{2,1,0:T(8,128)S(1)}, u32[]{:S(2)}, u32[]{:S(2)}) %collective-permute-start.1) | collective-permute-done | bytes 131104 | tf_op jit(solution)/shard_map/while/body/eval_jaxpr/ppermute | solution.py:27
  193.2 1.9 collective-permute-start.2
  195.2 4.4 %collective-permute-done.2 = f32[2,128,128]{2,1,0:T(8,128)S(1)} collective-permute-done((f32[2,128,128]{2,1,0:T(8,128)S(1)}, f32[2,128,128]{2,1,0:T(8,128)S(1)}, u32[]{:S(2)}, u32[]{:S(2)}) %collective-permute-start.2) | collective-permute-done | bytes 131104 | tf_op jit(solution)/shard_map/while/body/eval_jaxpr/ppermute | solution.py:35
  199.9 1.3 collective-permute-start.6
  201.2 4.6 %collective-permute-start.5 = (f32[2,128,128]{2,1,0:T(8,128)S(1)}, f32[2,128,128]{2,1,0:T(8,128)S(1)}, u32[]{:S(2)}, u32[]{:S(2)}) collective-permute-start(f32[2,128,128]{2,1,0:T(8,128)S(1)} %get-tuple-element.121), channel_id=1, source_target_pairs={{0,1},{1,2},{2,3},{4,5},{5,6},{6,7},{8,9},{9,10},{10,11},{12,13},{... | collective-permute-start | bytes 393224 | tf_op jit(solution)/shard_map/ppermute | solution.py:26
  206.3 2.8 %collective-permute-done.5 = f32[2,128,128]{2,1,0:T(8,128)S(1)} collective-permute-done((f32[2,128,128]{2,1,0:T(8,128)S(1)}, f32[2,128,128]{2,1,0:T(8,128)S(1)}, u32[]{:S(2)}, u32[]{:S(2)}) %collective-permute-start.5) | collective-permute-done | bytes 131104 | tf_op jit(solution)/shard_map/ppermute | solution.py:26
  213.5 4.4 %collective-permute-start.8 = (f32[3,1,256,256]{3,2,1,0:T(8,128)S(1)}, f32[3,1,256,256]{3,2,1,0:T(8,128)S(1)}, u32[]{:S(2)}, u32[]{:S(2)}) collective-permute-start(f32[3,1,256,256]{3,2,1,0:T(8,128)S(1)} %get-tuple-element.159), channel_id=1, source_target_pairs={{0,1},{1,2},{2,3},{4,5},{5,6},{6,7},{8,9},{9,10},{10,11},{12,13},{... | collective-permute-start | bytes 2359304 | tf_op jit(solution)/shard_map/ppermute | solution.py:26
  217.9 1.5 collective-permute-start.7
  219.4 1.7 fusion.133
  222.1 12.3 %collective-permute-done.8 = f32[3,1,256,256]{3,2,1,0:T(8,128)S(1)} collective-permute-done((f32[3,1,256,256]{3,2,1,0:T(8,128)S(1)}, f32[3,1,256,256]{3,2,1,0:T(8,128)S(1)}, u32[]{:S(2)}, u32[]{:S(2)}) %collective-permute-start.8) | collective-permute-done | bytes 786464 | tf_op jit(solution)/shard_map/ppermute | solution.py:26
  234.4 4.2 %collective-permute-done.7 = f32[3,1,256,256]{3,2,1,0:T(8,128)S(1)} collective-permute-done((f32[3,1,256,256]{3,2,1,0:T(8,128)S(1)}, f32[3,1,256,256]{3,2,1,0:T(8,128)S(1)}, u32[]{:S(2)}, u32[]{:S(2)}) %collective-permute-start.7) | collective-permute-done | bytes 786464 | tf_op jit(solution)/shard_map/ppermute | solution.py:27
  239.5 6.1 %add_add_fusion = f32[3,4,256,256]{3,2,1,0:T(8,128)S(1)} fusion(f32[3,4,256,255]{3,2,1,0:T(8,128)S(1)} %get-tuple-element.166, f32[3,4,256,1]{3,2,1,0:T(8,128)} %get-tuple-element.168, f32[3,4,256,1]{3,2,1,0:T(8,128)S(1)} %get-tuple-element.167, f32[3,4,256,255]{3,2,1,0:T(8,128)S(1)} %get-tuple-element.165, f32[3,4,255,256]{3,2,1,0:T(8,128)S(1)} %get-tuple-element.162, ...), kind=kLoop, calls=%fused_computation.38 | loop fusion | flops 28311552 | bytes 22544384 | tf_op jit(solution)/shard_map/add | solution.py:53
  246.4 2.2 collective-permute-start.10
  248.6 1.3 collective-permute-start.9
  250.1 2.7 %collective-permute-done.10 = f32[1,256,256]{2,1,0:T(8,128)S(1)} collective-permute-done((f32[1,256,256]{2,1,0:T(8,128)S(1)}, f32[1,256,256]{2,1,0:T(8,128)S(1)}, u32[]{:S(2)}, u32[]{:S(2)}) %collective-permute-start.10) | collective-permute-done | bytes 262176 | tf_op jit(solution)/shard_map/ppermute | solution.py:26
  252.8 4.1 %collective-permute-done.9 = f32[1,256,256]{2,1,0:T(8,128)S(1)} collective-permute-done((f32[1,256,256]{2,1,0:T(8,128)S(1)}, f32[1,256,256]{2,1,0:T(8,128)S(1)}, u32[]{:S(2)}, u32[]{:S(2)}) %collective-permute-start.9) | collective-permute-done | bytes 262176 | tf_op jit(solution)/shard_map/ppermute | solution.py:27
  256.9 2.0 fusion.10
  259.0 1.5 maximum_bitcast_fusion
  (173 shorter events, 21.3 us)
Async XLA Ops:
  6.5 9.0 %copy-start = (f32[1,4,256,256]{3,2,1,0:T(8,128)S(1)}, f32[1,4,256,256]{3,2,1,0:T(8,128)}, u32[]{:S(2)}) copy-start(f32[1,4,256,256]{3,2,1,0:T(8,128)} %param.5) | copy-start | bytes 3145732
  6.5 68.4 %all-reduce.2.cloned.1.call-start = ((), (), s32[]{:S(2)}) async-start(), calls=%async_computation | async-start | bytes 2097152 | tf_op jit(solution)/shard_map/psum | solution.py:16
  8.6 12.5 %copy-start.4 = (f32[128,2,128]{2,0,1:T(8,128)}, f32[128,2,128]{2,0,1:T(8,128)S(1)}, u32[]{:S(2)}) copy-start(f32[128,2,128]{2,0,1:T(8,128)S(1)} %convolution_multiply_fusion.1) | copy-start | bytes 393220
  10.7 7.4 %collective-permute-start.3 = (f32[2,1,128,128]{3,2,1,0:T(8,128)S(1)}, f32[2,1,128,128]{3,2,1,0:T(8,128)S(1)}, u32[]{:S(2)}, u32[]{:S(2)}) collective-permute-start(f32[2,1,128,128]{3,2,1,0:T(8,128)S(1)} %get-tuple-element.197), channel_id=1, source_target_pairs={{0,1},{1,2},{2,3},{4,5},{5,6},{6,7},{8,9},{9,10},{10,11},{12,13},{... | collective-permute-start | bytes 393224 | tf_op jit(solution)/shard_map/ppermute | solution.py:26
  14.2 6.9 %collective-permute-start.4 = (f32[2,1,128,128]{3,2,1,0:T(8,128)S(1)}, f32[2,1,128,128]{3,2,1,0:T(8,128)S(1)}, u32[]{:S(2)}, u32[]{:S(2)}) collective-permute-start(f32[2,1,128,128]{3,2,1,0:T(8,128)S(1)} %get-tuple-element.198), channel_id=1, source_target_pairs={{1,0},{2,1},{3,2},{5,4},{6,5},{7,6},{9,8},{10,9},{11,10},{13,12},{... | collective-permute-start | bytes 393224 | tf_op jit(solution)/shard_map/ppermute | solution.py:27
  77.0 129.2 %copy-start.3 = (f32[4,256,256]{2,1,0:T(8,128)S(1)}, f32[4,256,256]{2,1,0:T(8,128)}, u32[]{:S(2)}) copy-start(f32[4,256,256]{2,1,0:T(8,128)} %all-reduce.2.cloned.1.call-done) | copy-start | bytes 3145732
  77.0 6.0 %collective-permute-start = (f32[2,128,128]{2,1,0:T(8,128)S(1)}, f32[2,128,128]{2,1,0:T(8,128)S(1)}, u32[]{:S(2)}, u32[]{:S(2)}) collective-permute-start(f32[2,128,128]{2,1,0:T(8,128)S(1)} %get-tuple-element.307), channel_id=1, source_target_pairs={{0,1},{1,2},{2,3},{4,5},{5,6},{6,7},{8,9},{9,10},{10,11},{12,13},{... | collective-permute-start | bytes 393224 | tf_op jit(solution)/shard_map/while/body/eval_jaxpr/ppermute | solution.py:26
  80.5 6.9 %collective-permute-start.1 = (f32[2,128,128]{2,1,0:T(8,128)S(1)}, f32[2,128,128]{2,1,0:T(8,128)S(1)}, u32[]{:S(2)}, u32[]{:S(2)}) collective-permute-start(f32[2,128,128]{2,1,0:T(8,128)S(1)} %get-tuple-element.307), channel_id=1, source_target_pairs={{1,0},{2,1},{3,2},{5,4},{6,5},{7,6},{9,8},{10,9},{11,10},{13,12},{... | collective-permute-start | bytes 393224 | tf_op jit(solution)/shard_map/while/body/eval_jaxpr/ppermute | solution.py:27
  88.6 6.3 %collective-permute-start.2 = (f32[2,128,128]{2,1,0:T(8,128)S(1)}, f32[2,128,128]{2,1,0:T(8,128)S(1)}, u32[]{:S(2)}, u32[]{:S(2)}) collective-permute-start(f32[2,128,128]{2,1,0:T(8,128)S(1)} %fusion.173), channel_id=1, source_target_pairs={{0,4},{4,8},{8,12},{12,16},{16,20},{20,24},{24,28},{1,5},{5,9},{9,... | collective-permute-start | bytes 393224 | tf_op jit(solution)/shard_map/while/body/eval_jaxpr/ppermute | solution.py:35
  94.9 5.9 %collective-permute-start = (f32[2,128,128]{2,1,0:T(8,128)S(1)}, f32[2,128,128]{2,1,0:T(8,128)S(1)}, u32[]{:S(2)}, u32[]{:S(2)}) collective-permute-start(f32[2,128,128]{2,1,0:T(8,128)S(1)} %get-tuple-element.307), channel_id=1, source_target_pairs={{0,1},{1,2},{2,3},{4,5},{5,6},{6,7},{8,9},{9,10},{10,11},{12,13},{... | collective-permute-start | bytes 393224 | tf_op jit(solution)/shard_map/while/body/eval_jaxpr/ppermute | solution.py:26
  98.3 6.9 %collective-permute-start.1 = (f32[2,128,128]{2,1,0:T(8,128)S(1)}, f32[2,128,128]{2,1,0:T(8,128)S(1)}, u32[]{:S(2)}, u32[]{:S(2)}) collective-permute-start(f32[2,128,128]{2,1,0:T(8,128)S(1)} %get-tuple-element.307), channel_id=1, source_target_pairs={{1,0},{2,1},{3,2},{5,4},{6,5},{7,6},{9,8},{10,9},{11,10},{13,12},{... | collective-permute-start | bytes 393224 | tf_op jit(solution)/shard_map/while/body/eval_jaxpr/ppermute | solution.py:27
  106.4 6.3 %collective-permute-start.2 = (f32[2,128,128]{2,1,0:T(8,128)S(1)}, f32[2,128,128]{2,1,0:T(8,128)S(1)}, u32[]{:S(2)}, u32[]{:S(2)}) collective-permute-start(f32[2,128,128]{2,1,0:T(8,128)S(1)} %fusion.173), channel_id=1, source_target_pairs={{0,4},{4,8},{8,12},{12,16},{16,20},{20,24},{24,28},{1,5},{5,9},{9,... | collective-permute-start | bytes 393224 | tf_op jit(solution)/shard_map/while/body/eval_jaxpr/ppermute | solution.py:35
  112.7 6.3 %collective-permute-start = (f32[2,128,128]{2,1,0:T(8,128)S(1)}, f32[2,128,128]{2,1,0:T(8,128)S(1)}, u32[]{:S(2)}, u32[]{:S(2)}) collective-permute-start(f32[2,128,128]{2,1,0:T(8,128)S(1)} %get-tuple-element.307), channel_id=1, source_target_pairs={{0,1},{1,2},{2,3},{4,5},{5,6},{6,7},{8,9},{9,10},{10,11},{12,13},{... | collective-permute-start | bytes 393224 | tf_op jit(solution)/shard_map/while/body/eval_jaxpr/ppermute | solution.py:26
  116.1 7.0 %collective-permute-start.1 = (f32[2,128,128]{2,1,0:T(8,128)S(1)}, f32[2,128,128]{2,1,0:T(8,128)S(1)}, u32[]{:S(2)}, u32[]{:S(2)}) collective-permute-start(f32[2,128,128]{2,1,0:T(8,128)S(1)} %get-tuple-element.307), channel_id=1, source_target_pairs={{1,0},{2,1},{3,2},{5,4},{6,5},{7,6},{9,8},{10,9},{11,10},{13,12},{... | collective-permute-start | bytes 393224 | tf_op jit(solution)/shard_map/while/body/eval_jaxpr/ppermute | solution.py:27
  124.4 6.3 %collective-permute-start.2 = (f32[2,128,128]{2,1,0:T(8,128)S(1)}, f32[2,128,128]{2,1,0:T(8,128)S(1)}, u32[]{:S(2)}, u32[]{:S(2)}) collective-permute-start(f32[2,128,128]{2,1,0:T(8,128)S(1)} %fusion.173), channel_id=1, source_target_pairs={{0,4},{4,8},{8,12},{12,16},{16,20},{20,24},{24,28},{1,5},{5,9},{9,... | collective-permute-start | bytes 393224 | tf_op jit(solution)/shard_map/while/body/eval_jaxpr/ppermute | solution.py:35
  130.7 5.6 %collective-permute-start = (f32[2,128,128]{2,1,0:T(8,128)S(1)}, f32[2,128,128]{2,1,0:T(8,128)S(1)}, u32[]{:S(2)}, u32[]{:S(2)}) collective-permute-start(f32[2,128,128]{2,1,0:T(8,128)S(1)} %get-tuple-element.307), channel_id=1, source_target_pairs={{0,1},{1,2},{2,3},{4,5},{5,6},{6,7},{8,9},{9,10},{10,11},{12,13},{... | collective-permute-start | bytes 393224 | tf_op jit(solution)/shard_map/while/body/eval_jaxpr/ppermute | solution.py:26
  132.9 7.5 %collective-permute-start.1 = (f32[2,128,128]{2,1,0:T(8,128)S(1)}, f32[2,128,128]{2,1,0:T(8,128)S(1)}, u32[]{:S(2)}, u32[]{:S(2)}) collective-permute-start(f32[2,128,128]{2,1,0:T(8,128)S(1)} %get-tuple-element.307), channel_id=1, source_target_pairs={{1,0},{2,1},{3,2},{5,4},{6,5},{7,6},{9,8},{10,9},{11,10},{13,12},{... | collective-permute-start | bytes 393224 | tf_op jit(solution)/shard_map/while/body/eval_jaxpr/ppermute | solution.py:27
  141.6 6.3 %collective-permute-start.2 = (f32[2,128,128]{2,1,0:T(8,128)S(1)}, f32[2,128,128]{2,1,0:T(8,128)S(1)}, u32[]{:S(2)}, u32[]{:S(2)}) collective-permute-start(f32[2,128,128]{2,1,0:T(8,128)S(1)} %fusion.173), channel_id=1, source_target_pairs={{0,4},{4,8},{8,12},{12,16},{16,20},{20,24},{24,28},{1,5},{5,9},{9,... | collective-permute-start | bytes 393224 | tf_op jit(solution)/shard_map/while/body/eval_jaxpr/ppermute | solution.py:35
  147.9 5.6 %collective-permute-start = (f32[2,128,128]{2,1,0:T(8,128)S(1)}, f32[2,128,128]{2,1,0:T(8,128)S(1)}, u32[]{:S(2)}, u32[]{:S(2)}) collective-permute-start(f32[2,128,128]{2,1,0:T(8,128)S(1)} %get-tuple-element.307), channel_id=1, source_target_pairs={{0,1},{1,2},{2,3},{4,5},{5,6},{6,7},{8,9},{9,10},{10,11},{12,13},{... | collective-permute-start | bytes 393224 | tf_op jit(solution)/shard_map/while/body/eval_jaxpr/ppermute | solution.py:26
  150.1 7.5 %collective-permute-start.1 = (f32[2,128,128]{2,1,0:T(8,128)S(1)}, f32[2,128,128]{2,1,0:T(8,128)S(1)}, u32[]{:S(2)}, u32[]{:S(2)}) collective-permute-start(f32[2,128,128]{2,1,0:T(8,128)S(1)} %get-tuple-element.307), channel_id=1, source_target_pairs={{1,0},{2,1},{3,2},{5,4},{6,5},{7,6},{9,8},{10,9},{11,10},{13,12},{... | collective-permute-start | bytes 393224 | tf_op jit(solution)/shard_map/while/body/eval_jaxpr/ppermute | solution.py:27
  158.8 6.3 %collective-permute-start.2 = (f32[2,128,128]{2,1,0:T(8,128)S(1)}, f32[2,128,128]{2,1,0:T(8,128)S(1)}, u32[]{:S(2)}, u32[]{:S(2)}) collective-permute-start(f32[2,128,128]{2,1,0:T(8,128)S(1)} %fusion.173), channel_id=1, source_target_pairs={{0,4},{4,8},{8,12},{12,16},{16,20},{20,24},{24,28},{1,5},{5,9},{9,... | collective-permute-start | bytes 393224 | tf_op jit(solution)/shard_map/while/body/eval_jaxpr/ppermute | solution.py:35
  165.1 5.6 %collective-permute-start = (f32[2,128,128]{2,1,0:T(8,128)S(1)}, f32[2,128,128]{2,1,0:T(8,128)S(1)}, u32[]{:S(2)}, u32[]{:S(2)}) collective-permute-start(f32[2,128,128]{2,1,0:T(8,128)S(1)} %get-tuple-element.307), channel_id=1, source_target_pairs={{0,1},{1,2},{2,3},{4,5},{5,6},{6,7},{8,9},{9,10},{10,11},{12,13},{... | collective-permute-start | bytes 393224 | tf_op jit(solution)/shard_map/while/body/eval_jaxpr/ppermute | solution.py:26
  167.3 7.5 %collective-permute-start.1 = (f32[2,128,128]{2,1,0:T(8,128)S(1)}, f32[2,128,128]{2,1,0:T(8,128)S(1)}, u32[]{:S(2)}, u32[]{:S(2)}) collective-permute-start(f32[2,128,128]{2,1,0:T(8,128)S(1)} %get-tuple-element.307), channel_id=1, source_target_pairs={{1,0},{2,1},{3,2},{5,4},{6,5},{7,6},{9,8},{10,9},{11,10},{13,12},{... | collective-permute-start | bytes 393224 | tf_op jit(solution)/shard_map/while/body/eval_jaxpr/ppermute | solution.py:27
  176.0 6.3 %collective-permute-start.2 = (f32[2,128,128]{2,1,0:T(8,128)S(1)}, f32[2,128,128]{2,1,0:T(8,128)S(1)}, u32[]{:S(2)}, u32[]{:S(2)}) collective-permute-start(f32[2,128,128]{2,1,0:T(8,128)S(1)} %fusion.173), channel_id=1, source_target_pairs={{0,4},{4,8},{8,12},{12,16},{16,20},{20,24},{24,28},{1,5},{5,9},{9,... | collective-permute-start | bytes 393224 | tf_op jit(solution)/shard_map/while/body/eval_jaxpr/ppermute | solution.py:35
  182.3 5.6 %collective-permute-start = (f32[2,128,128]{2,1,0:T(8,128)S(1)}, f32[2,128,128]{2,1,0:T(8,128)S(1)}, u32[]{:S(2)}, u32[]{:S(2)}) collective-permute-start(f32[2,128,128]{2,1,0:T(8,128)S(1)} %get-tuple-element.307), channel_id=1, source_target_pairs={{0,1},{1,2},{2,3},{4,5},{5,6},{6,7},{8,9},{9,10},{10,11},{12,13},{... | collective-permute-start | bytes 393224 | tf_op jit(solution)/shard_map/while/body/eval_jaxpr/ppermute | solution.py:26
  184.5 7.5 %collective-permute-start.1 = (f32[2,128,128]{2,1,0:T(8,128)S(1)}, f32[2,128,128]{2,1,0:T(8,128)S(1)}, u32[]{:S(2)}, u32[]{:S(2)}) collective-permute-start(f32[2,128,128]{2,1,0:T(8,128)S(1)} %get-tuple-element.307), channel_id=1, source_target_pairs={{1,0},{2,1},{3,2},{5,4},{6,5},{7,6},{9,8},{10,9},{11,10},{13,12},{... | collective-permute-start | bytes 393224 | tf_op jit(solution)/shard_map/while/body/eval_jaxpr/ppermute | solution.py:27
  193.2 6.3 %collective-permute-start.2 = (f32[2,128,128]{2,1,0:T(8,128)S(1)}, f32[2,128,128]{2,1,0:T(8,128)S(1)}, u32[]{:S(2)}, u32[]{:S(2)}) collective-permute-start(f32[2,128,128]{2,1,0:T(8,128)S(1)} %fusion.173), channel_id=1, source_target_pairs={{0,4},{4,8},{8,12},{12,16},{16,20},{20,24},{24,28},{1,5},{5,9},{9,... | collective-permute-start | bytes 393224 | tf_op jit(solution)/shard_map/while/body/eval_jaxpr/ppermute | solution.py:35
  199.9 9.3 %collective-permute-start.6 = (f32[2,128,128]{2,1,0:T(8,128)S(1)}, f32[2,128,128]{2,1,0:T(8,128)S(1)}, u32[]{:S(2)}, u32[]{:S(2)}) collective-permute-start(f32[2,128,128]{2,1,0:T(8,128)S(1)} %get-tuple-element.121), channel_id=1, source_target_pairs={{1,0},{2,1},{3,2},{5,4},{6,5},{7,6},{9,8},{10,9},{11,10},{13,12},{... | collective-permute-start | bytes 393224 | tf_op jit(solution)/shard_map/ppermute | solution.py:27
  201.2 7.9 %collective-permute-start.5 = (f32[2,128,128]{2,1,0:T(8,128)S(1)}, f32[2,128,128]{2,1,0:T(8,128)S(1)}, u32[]{:S(2)}, u32[]{:S(2)}) collective-permute-start(f32[2,128,128]{2,1,0:T(8,128)S(1)} %get-tuple-element.121), channel_id=1, source_target_pairs={{0,1},{1,2},{2,3},{4,5},{5,6},{6,7},{8,9},{9,10},{10,11},{12,13},{... | collective-permute-start | bytes 393224 | tf_op jit(solution)/shard_map/ppermute | solution.py:26
  209.5 0.9 copy-start.8
  209.6 1.6 copy-start.5
  213.5 21.0 %collective-permute-start.8 = (f32[3,1,256,256]{3,2,1,0:T(8,128)S(1)}, f32[3,1,256,256]{3,2,1,0:T(8,128)S(1)}, u32[]{:S(2)}, u32[]{:S(2)}) collective-permute-start(f32[3,1,256,256]{3,2,1,0:T(8,128)S(1)} %get-tuple-element.159), channel_id=1, source_target_pairs={{0,1},{1,2},{2,3},{4,5},{5,6},{6,7},{8,9},{9,10},{10,11},{12,13},{... | collective-permute-start | bytes 2359304 | tf_op jit(solution)/shard_map/ppermute | solution.py:26
  217.9 20.7 %collective-permute-start.7 = (f32[3,1,256,256]{3,2,1,0:T(8,128)S(1)}, f32[3,1,256,256]{3,2,1,0:T(8,128)S(1)}, u32[]{:S(2)}, u32[]{:S(2)}) collective-permute-start(f32[3,1,256,256]{3,2,1,0:T(8,128)S(1)} %get-tuple-element.160), channel_id=1, source_target_pairs={{1,0},{2,1},{3,2},{5,4},{6,5},{7,6},{9,8},{10,9},{11,10},{13,12},{... | collective-permute-start | bytes 2359304 | tf_op jit(solution)/shard_map/ppermute | solution.py:27
  221.1 18.4 %copy-start.1 = (f32[4,256,256]{2,1,0:T(8,128)S(1)}, f32[4,256,256]{2,1,0:T(8,128)}, u32[]{:S(2)}) copy-start(f32[4,256,256]{2,1,0:T(8,128)} %param.7) | copy-start | bytes 3145732
  221.1 18.4 %copy-start.2 = (f32[1,4,256,256]{3,2,1,0:T(8,128)S(1)}, f32[1,4,256,256]{3,2,1,0:T(8,128)}, u32[]{:S(2)}) copy-start(f32[1,4,256,256]{3,2,1,0:T(8,128)} %param.6) | copy-start | bytes 3145732
  234.4 4.2 %copy-start.6 = (f32[3,1,256,256]{3,2,1,0:T(8,128)}, f32[3,1,256,256]{3,2,1,0:T(8,128)S(1)}, u32[]{:S(2)}) copy-start(f32[3,1,256,256]{3,2,1,0:T(8,128)S(1)} %collective-permute-done.8) | copy-start | bytes 2359300
  238.6 0.9 copy-start.7
  246.4 6.4 %collective-permute-start.10 = (f32[1,256,256]{2,1,0:T(8,128)S(1)}, f32[1,256,256]{2,1,0:T(8,128)S(1)}, u32[]{:S(2)}, u32[]{:S(2)}) collective-permute-start(f32[1,256,256]{2,1,0:T(8,128)S(1)} %get-tuple-element.169), channel_id=1, source_target_pairs={{0,1},{1,2},{2,3},{4,5},{5,6},{6,7},{8,9},{9,10},{10,11},{12,13},{... | collective-permute-start | bytes 786440 | tf_op jit(solution)/shard_map/ppermute | solution.py:26
  248.6 8.3 %collective-permute-start.9 = (f32[1,256,256]{2,1,0:T(8,128)S(1)}, f32[1,256,256]{2,1,0:T(8,128)S(1)}, u32[]{:S(2)}, u32[]{:S(2)}) collective-permute-start(f32[1,256,256]{2,1,0:T(8,128)S(1)} %get-tuple-element.170), channel_id=1, source_target_pairs={{1,0},{2,1},{3,2},{5,4},{6,5},{7,6},{9,8},{10,9},{11,10},{13,12},{... | collective-permute-start | bytes 786440 | tf_op jit(solution)/shard_map/ppermute | solution.py:27
Sparse Core Ops, SparseCore 0:
  16.8 58.0 all-reduce.1
where the time goes:
time: 268 us; the launch traced here: 267 us
  waiting for transfers between devices  154 us (57%)
  starting transfers between devices  61.6 us (23%)
  other arithmetic  16.3 us (6%)
  between operations  13.9 us (5%)
  local copies, waits for them, and re-layouts  10.2 us (4%)
  matrix products  9.94 us (4%)
    psum x1, waiting for transfers between devices, broadcast(): return lax.psum(jnp.where(mine, array, jnp.zeros_like(array)), axis)  53.8 us
    ppermute x11, waiting for transfers between devices, padded_2(): after = lax.ppermute(first, axis, down)  40.2 us
    ppermute x11, starting transfers between devices, padded_2(): before = lax.ppermute(last, axis, up)  33.8 us
    ppermute x7, waiting for transfers between devices, shifted(): lax.ppermute(value, axis, [(source, source + steps) for source in range(f...  30.5 us
    ppermute x11, waiting for transfers between devices, padded_2(): before = lax.ppermute(last, axis, up)  29.9 us
    ppermute x11, starting transfers between devices, padded_2(): after = lax.ppermute(first, axis, down)  14.4 us
    ppermute x7, starting transfers between devices, shifted(): lax.ppermute(value, axis, [(source, source + steps) for source in range(f...  13.4 us
    slice x36, local copies, waits for them, and re-layouts, tendency(): plus_y = jnp.roll(middle, -1, axis=-1)  6.88 us
  transfers between devices with their start and end apart: 30, of which 28 were waited for; matrix products, arithmetic and copies ran while one was open for 2% of the time, Pallas kernels for 0%

commit v1 on v0

--- a/solution.py
+++ b/solution.py
@@ -13,7 +13,7 @@
 
 def broadcast(array, axis, root):
     mine = lax.axis_index(axis) == root
-    return lax.psum(jnp.where(mine, array, jnp.zeros_like(array)), axis)
+    return jnp.sum(lax.all_gather(jnp.where(mine, array, jnp.zeros_like(array)), axis), axis=0)
 
 
 def padded_2(array, sides, width):

time: 268 us -> 263 us (0.981)
  waiting for transfers between devices: 154 us -> 147 us
  other arithmetic: 16.3 us -> 21.3 us
  matrix products: 9.94 us -> 5.58 us
    psum x1 -> x0, waiting for transfers between devices: 53.8 us -> none  [broadcast(): return lax.psum(jnp.where(mine, array, jnp.zeros_like(array)), axis)]
    all_gather x0 -> x1, waiting for transfers between devices: none -> 44.4 us  [broadcast(): lax.all_gather(jnp.where(mine, array, jnp.zeros_like(array)), axis)]
    reduce_sum x0 -> x1, other arithmetic: none -> 4.06 us  [broadcast(): jnp.sum(lax.all_gather(jnp.where(mine, array, jnp.zeros_like(array)), axi...]
    dot_general x4, matrix products: 5.53 us -> 1.8 us  [restrict(): jnp.einsum('...xy,yb->...xb', summed_z, pair_table(count_y), precision=la...]
  transfers between devices with their start and end apart: 30 -> 30, of which waited for: 28 -> 29; matrix products, arithmetic and copies ran while one was open for 2% -> 3% of each run, Pallas kernels for 0% -> 0%
where the time goes in v1:
time: 263 us; the launch traced here: 262 us
  waiting for transfers between devices  147 us (56%)
  starting transfers between devices  61.4 us (23%)
  other arithmetic  21.3 us (8%)
  between operations  13.9 us (5%)
  local copies, waits for them, and re-layouts  11.8 us (4%)
  matrix products  5.58 us (2%)
    all_gather x1, waiting for transfers between devices, broadcast(): lax.all_gather(jnp.where(mine, array, jnp.zeros_like(array)), axis)  44.4 us
    ppermute x11, waiting for transfers between devices, padded_2(): after = lax.ppermute(first, axis, down)  41.3 us
    ppermute x11, starting transfers between devices, padded_2(): before = lax.ppermute(last, axis, up)  33.6 us
    ppermute x7, waiting for transfers between devices, shifted(): lax.ppermute(value, axis, [(source, source + steps) for source in range(f...  30.5 us
    ppermute x11, waiting for transfers between devices, padded_2(): before = lax.ppermute(last, axis, up)  30.3 us
    ppermute x11, starting transfers between devices, padded_2(): after = lax.ppermute(first, axis, down)  14.4 us
    ppermute x7, starting transfers between devices, shifted(): lax.ppermute(value, axis, [(source, source + steps) for source in range(f...  13.4 us
    slice x36, local copies, waits for them, and re-layouts, tendency(): plus_y = jnp.roll(middle, -1, axis=-1)  7.41 us
  transfers between devices with their start and end apart: 30, of which 29 were waited for; matrix products, arithmetic and copies ran while one was open for 3% of the time, Pallas kernels for 0%

profile of v1, /device:TPU:2, one launch (start us, length us, event | category | flops | bytes accessed | tf_op | source)
XLA Modules:
  0.0 261.6 jit_solution(78173513783469117)
XLA Ops:
  6.5 1.1 broadcast_select_fusion.1
  9.9 3.5 %collective-permute-start.3 = (f32[2,1,128,128]{3,2,1,0:T(8,128)S(1)}, f32[2,1,128,128]{3,2,1,0:T(8,128)S(1)}, u32[]{:S(2)}, u32[]{:S(2)}) collective-permute-start(f32[2,1,128,128]{3,2,1,0:T(8,128)S(1)} %get-tuple-element.197), channel_id=1, source_target_pairs={{0,1},{1,2},{2,3},{4,5},{5,6},{6,7},{8,9},{9,10},{10,11},{12,13},{... | collective-permute-start | bytes 393224 | tf_op jit(solution)/shard_map/ppermute | solution.py:26
  13.4 1.3 collective-permute-start.4
  16.1 4.1 %collective-permute-done.4 = f32[2,1,128,128]{3,2,1,0:T(8,128)S(1)} collective-permute-done((f32[2,1,128,128]{3,2,1,0:T(8,128)S(1)}, f32[2,1,128,128]{3,2,1,0:T(8,128)S(1)}, u32[]{:S(2)}, u32[]{:S(2)}) %collective-permute-start.4) | collective-permute-done | bytes 131104 | tf_op jit(solution)/shard_map/ppermute | solution.py:27
  20.3 44.4 %all-gather.2.cloned.1.call-done = f32[8,4,256,256]{3,2,1,0:T(8,128)} async-done(((f32[1,4,256,256]{3,2,1,0:T(8,128)}), f32[8,4,256,256]{3,2,1,0:T(8,128)}) %all-gather.2.cloned.1.call-update) | async-done | bytes 8388624 | tf_op jit(solution)/shard_map/all_gather | solution.py:16
  64.7 4.1 %reduce_sum.11 = f32[4,256,256]{2,1,0:T(8,128)S(1)} reduce(f32[8,4,256,256]{3,2,1,0:T(8,128)} %all-gather.2.cloned.1.call-done, f32[]{:T(128)} %constant.227.clone.1), dimensions={0}, to_apply=%region_0.1 | reduce | flops 1835008 | bytes 9437188 | tf_op jit(solution)/shard_map/reduce_sum | solution.py:16
  69.6 122.5 %while.13 = (s32[]{:T(128)}, f32[2,128,128]{2,1,0:T(8,128)S(1)}, pred[]{:T(512)}, f32[2,4,128,128]{3,2,1,0:T(8,128)S(1)}, f32[2,128,128]{2,1,0:T(8,128)S(1)}, /*...) while((s32[]{:T(128)}, f32[2,128,128]{2,1,0:T(8,128)S(1)}, ...), condition=%wide.region_2.3_spmd, body=%wide.region_1.2_spmd.sunk | while | flops 3047446 | bytes 10354974 | solution.py:134
  69.7 3.4 %collective-permute-start = (f32[2,128,128]{2,1,0:T(8,128)S(1)}, f32[2,128,128]{2,1,0:T(8,128)S(1)}, u32[]{:S(2)}, u32[]{:S(2)}) collective-permute-start(f32[2,128,128]{2,1,0:T(8,128)S(1)} %get-tuple-element.308), channel_id=1, source_target_pairs={{0,1},{1,2},{2,3},{4,5},{5,6},{6,7},{8,9},{9,10},{10,11},{12,13},{... | collective-permute-start | bytes 393224 | tf_op jit(solution)/shard_map/while/body/eval_jaxpr/ppermute | solution.py:26
  73.1 1.3 collective-permute-start.1
  74.4 1.8 collective-permute-done
  76.3 4.1 %collective-permute-done.1 = f32[2,128,128]{2,1,0:T(8,128)S(1)} collective-permute-done((f32[2,128,128]{2,1,0:T(8,128)S(1)}, f32[2,128,128]{2,1,0:T(8,128)S(1)}, u32[]{:S(2)}, u32[]{:S(2)}) %collective-permute-start.1) | collective-permute-done | bytes 131104 | tf_op jit(solution)/shard_map/while/body/eval_jaxpr/ppermute | solution.py:27
  81.5 1.9 collective-permute-start.2
  83.5 4.4 %collective-permute-done.2 = f32[2,128,128]{2,1,0:T(8,128)S(1)} collective-permute-done((f32[2,128,128]{2,1,0:T(8,128)S(1)}, f32[2,128,128]{2,1,0:T(8,128)S(1)}, u32[]{:S(2)}, u32[]{:S(2)}) %collective-permute-start.2) | collective-permute-done | bytes 131104 | tf_op jit(solution)/shard_map/while/body/eval_jaxpr/ppermute | solution.py:35
  87.9 3.4 %collective-permute-start = (f32[2,128,128]{2,1,0:T(8,128)S(1)}, f32[2,128,128]{2,1,0:T(8,128)S(1)}, u32[]{:S(2)}, u32[]{:S(2)}) collective-permute-start(f32[2,128,128]{2,1,0:T(8,128)S(1)} %get-tuple-element.308), channel_id=1, source_target_pairs={{0,1},{1,2},{2,3},{4,5},{5,6},{6,7},{8,9},{9,10},{10,11},{12,13},{... | collective-permute-start | bytes 393224 | tf_op jit(solution)/shard_map/while/body/eval_jaxpr/ppermute | solution.py:26
  91.3 1.3 collective-permute-start.1
  92.6 1.2 collective-permute-done
  93.8 4.3 %collective-permute-done.1 = f32[2,128,128]{2,1,0:T(8,128)S(1)} collective-permute-done((f32[2,128,128]{2,1,0:T(8,128)S(1)}, f32[2,128,128]{2,1,0:T(8,128)S(1)}, u32[]{:S(2)}, u32[]{:S(2)}) %collective-permute-start.1) | collective-permute-done | bytes 131104 | tf_op jit(solution)/shard_map/while/body/eval_jaxpr/ppermute | solution.py:27
  99.3 1.9 collective-permute-start.2
  101.3 4.4 %collective-permute-done.2 = f32[2,128,128]{2,1,0:T(8,128)S(1)} collective-permute-done((f32[2,128,128]{2,1,0:T(8,128)S(1)}, f32[2,128,128]{2,1,0:T(8,128)S(1)}, u32[]{:S(2)}, u32[]{:S(2)}) %collective-permute-start.2) | collective-permute-done | bytes 131104 | tf_op jit(solution)/shard_map/while/body/eval_jaxpr/ppermute | solution.py:35
  105.7 3.4 %collective-permute-start = (f32[2,128,128]{2,1,0:T(8,128)S(1)}, f32[2,128,128]{2,1,0:T(8,128)S(1)}, u32[]{:S(2)}, u32[]{:S(2)}) collective-permute-start(f32[2,128,128]{2,1,0:T(8,128)S(1)} %get-tuple-element.308), channel_id=1, source_target_pairs={{0,1},{1,2},{2,3},{4,5},{5,6},{6,7},{8,9},{9,10},{10,11},{12,13},{... | collective-permute-start | bytes 393224 | tf_op jit(solution)/shard_map/while/body/eval_jaxpr/ppermute | solution.py:26
  109.1 1.3 collective-permute-start.1
  110.4 1.3 collective-permute-done
  111.7 4.2 %collective-permute-done.1 = f32[2,128,128]{2,1,0:T(8,128)S(1)} collective-permute-done((f32[2,128,128]{2,1,0:T(8,128)S(1)}, f32[2,128,128]{2,1,0:T(8,128)S(1)}, u32[]{:S(2)}, u32[]{:S(2)}) %collective-permute-start.1) | collective-permute-done | bytes 131104 | tf_op jit(solution)/shard_map/while/body/eval_jaxpr/ppermute | solution.py:27
  117.1 1.9 collective-permute-start.2
  119.1 4.4 %collective-permute-done.2 = f32[2,128,128]{2,1,0:T(8,128)S(1)} collective-permute-done((f32[2,128,128]{2,1,0:T(8,128)S(1)}, f32[2,128,128]{2,1,0:T(8,128)S(1)}, u32[]{:S(2)}, u32[]{:S(2)}) %collective-permute-start.2) | collective-permute-done | bytes 131104 | tf_op jit(solution)/shard_map/while/body/eval_jaxpr/ppermute | solution.py:35
  123.5 2.0 collective-permute-start
  125.5 1.3 collective-permute-start.1
  126.8 2.0 collective-permute-done
  128.9 4.1 %collective-permute-done.1 = f32[2,128,128]{2,1,0:T(8,128)S(1)} collective-permute-done((f32[2,128,128]{2,1,0:T(8,128)S(1)}, f32[2,128,128]{2,1,0:T(8,128)S(1)}, u32[]{:S(2)}, u32[]{:S(2)}) %collective-permute-start.1) | collective-permute-done | bytes 131104 | tf_op jit(solution)/shard_map/while/body/eval_jaxpr/ppermute | solution.py:27
  134.2 1.9 collective-permute-start.2
  136.1 4.4 %collective-permute-done.2 = f32[2,128,128]{2,1,0:T(8,128)S(1)} collective-permute-done((f32[2,128,128]{2,1,0:T(8,128)S(1)}, f32[2,128,128]{2,1,0:T(8,128)S(1)}, u32[]{:S(2)}, u32[]{:S(2)}) %collective-permute-start.2) | collective-permute-done | bytes 131104 | tf_op jit(solution)/shard_map/while/body/eval_jaxpr/ppermute | solution.py:35
  140.5 2.2 collective-permute-start
  142.7 1.3 collective-permute-start.1
  144.0 2.0 collective-permute-done
  146.1 4.1 %collective-permute-done.1 = f32[2,128,128]{2,1,0:T(8,128)S(1)} collective-permute-done((f32[2,128,128]{2,1,0:T(8,128)S(1)}, f32[2,128,128]{2,1,0:T(8,128)S(1)}, u32[]{:S(2)}, u32[]{:S(2)}) %collective-permute-start.1) | collective-permute-done | bytes 131104 | tf_op jit(solution)/shard_map/while/body/eval_jaxpr/ppermute | solution.py:27
  151.4 1.9 collective-permute-start.2
  153.3 4.4 %collective-permute-done.2 = f32[2,128,128]{2,1,0:T(8,128)S(1)} collective-permute-done((f32[2,128,128]{2,1,0:T(8,128)S(1)}, f32[2,128,128]{2,1,0:T(8,128)S(1)}, u32[]{:S(2)}, u32[]{:S(2)}) %collective-permute-start.2) | collective-permute-done | bytes 131104 | tf_op jit(solution)/shard_map/while/body/eval_jaxpr/ppermute | solution.py:35
  157.7 2.2 collective-permute-start
  159.9 1.3 collective-permute-start.1
  161.3 2.0 collective-permute-done
  163.4 4.1 %collective-permute-done.1 = f32[2,128,128]{2,1,0:T(8,128)S(1)} collective-permute-done((f32[2,128,128]{2,1,0:T(8,128)S(1)}, f32[2,128,128]{2,1,0:T(8,128)S(1)}, u32[]{:S(2)}, u32[]{:S(2)}) %collective-permute-start.1) | collective-permute-done | bytes 131104 | tf_op jit(solution)/shard_map/while/body/eval_jaxpr/ppermute | solution.py:27
  168.6 1.9 collective-permute-start.2
  170.6 4.4 %collective-permute-done.2 = f32[2,128,128]{2,1,0:T(8,128)S(1)} collective-permute-done((f32[2,128,128]{2,1,0:T(8,128)S(1)}, f32[2,128,128]{2,1,0:T(8,128)S(1)}, u32[]{:S(2)}, u32[]{:S(2)}) %collective-permute-start.2) | collective-permute-done | bytes 131104 | tf_op jit(solution)/shard_map/while/body/eval_jaxpr/ppermute | solution.py:35
  175.0 2.2 collective-permute-start
  177.2 1.3 collective-permute-start.1
  178.5 2.0 collective-permute-done
  180.6 4.1 %collective-permute-done.1 = f32[2,128,128]{2,1,0:T(8,128)S(1)} collective-permute-done((f32[2,128,128]{2,1,0:T(8,128)S(1)}, f32[2,128,128]{2,1,0:T(8,128)S(1)}, u32[]{:S(2)}, u32[]{:S(2)}) %collective-permute-start.1) | collective-permute-done | bytes 131104 | tf_op jit(solution)/shard_map/while/body/eval_jaxpr/ppermute | solution.py:27
  185.9 1.9 collective-permute-start.2
  187.8 4.4 %collective-permute-done.2 = f32[2,128,128]{2,1,0:T(8,128)S(1)} collective-permute-done((f32[2,128,128]{2,1,0:T(8,128)S(1)}, f32[2,128,128]{2,1,0:T(8,128)S(1)}, u32[]{:S(2)}, u32[]{:S(2)}) %collective-permute-start.2) | collective-permute-done | bytes 131104 | tf_op jit(solution)/shard_map/while/body/eval_jaxpr/ppermute | solution.py:35
  192.5 1.3 collective-permute-start.6
  193.8 4.6 %collective-permute-start.5 = (f32[2,128,128]{2,1,0:T(8,128)S(1)}, f32[2,128,128]{2,1,0:T(8,128)S(1)}, u32[]{:S(2)}, u32[]{:S(2)}) collective-permute-start(f32[2,128,128]{2,1,0:T(8,128)S(1)} %get-tuple-element.121), channel_id=1, source_target_pairs={{0,1},{1,2},{2,3},{4,5},{5,6},{6,7},{8,9},{9,10},{10,11},{12,13},{... | collective-permute-start | bytes 393224 | tf_op jit(solution)/shard_map/ppermute | solution.py:26
  198.8 2.9 %collective-permute-done.5 = f32[2,128,128]{2,1,0:T(8,128)S(1)} collective-permute-done((f32[2,128,128]{2,1,0:T(8,128)S(1)}, f32[2,128,128]{2,1,0:T(8,128)S(1)}, u32[]{:S(2)}, u32[]{:S(2)}) %collective-permute-start.5) | collective-permute-done | bytes 131104 | tf_op jit(solution)/shard_map/ppermute | solution.py:26
  206.7 4.4 %collective-permute-start.8 = (f32[3,1,256,256]{3,2,1,0:T(8,128)S(1)}, f32[3,1,256,256]{3,2,1,0:T(8,128)S(1)}, u32[]{:S(2)}, u32[]{:S(2)}) collective-permute-start(f32[3,1,256,256]{3,2,1,0:T(8,128)S(1)} %get-tuple-element.159), channel_id=1, source_target_pairs={{0,1},{1,2},{2,3},{4,5},{5,6},{6,7},{8,9},{9,10},{10,11},{12,13},{... | collective-permute-start | bytes 2359304 | tf_op jit(solution)/shard_map/ppermute | solution.py:26
  211.1 1.5 collective-permute-start.7
  212.6 2.2 fusion.134
  215.9 11.7 %collective-permute-done.8 = f32[3,1,256,256]{3,2,1,0:T(8,128)S(1)} collective-permute-done((f32[3,1,256,256]{3,2,1,0:T(8,128)S(1)}, f32[3,1,256,256]{3,2,1,0:T(8,128)S(1)}, u32[]{:S(2)}, u32[]{:S(2)}) %collective-permute-start.8) | collective-permute-done | bytes 786464 | tf_op jit(solution)/shard_map/ppermute | solution.py:26
  227.6 4.2 %collective-permute-done.7 = f32[3,1,256,256]{3,2,1,0:T(8,128)S(1)} collective-permute-done((f32[3,1,256,256]{3,2,1,0:T(8,128)S(1)}, f32[3,1,256,256]{3,2,1,0:T(8,128)S(1)}, u32[]{:S(2)}, u32[]{:S(2)}) %collective-permute-start.7) | collective-permute-done | bytes 786464 | tf_op jit(solution)/shard_map/ppermute | solution.py:27
  232.7 6.5 %add_add_fusion = f32[3,4,256,256]{3,2,1,0:T(8,128)S(1)} fusion(f32[3,4,256,255]{3,2,1,0:T(8,128)S(1)} %get-tuple-element.166, f32[3,4,256,1]{3,2,1,0:T(8,128)} %get-tuple-element.168, f32[3,4,256,1]{3,2,1,0:T(8,128)} %get-tuple-element.167, f32[3,4,256,255]{3,2,1,0:T(8,128)S(1)} %get-tuple-element.165, f32[3,4,255,256]{3,2,1,0:T(8,128)S(1)} %get-tuple-element.162, ...), kind=kLoop, calls=%fused_computation.38 | loop fusion | flops 28311552 | bytes 22544384 | tf_op jit(solution)/shard_map/add | solution.py:53
  240.6 2.3 collective-permute-start.10
  242.9 1.3 collective-permute-start.9
  244.4 2.7 %collective-permute-done.10 = f32[1,256,256]{2,1,0:T(8,128)S(1)} collective-permute-done((f32[1,256,256]{2,1,0:T(8,128)S(1)}, f32[1,256,256]{2,1,0:T(8,128)S(1)}, u32[]{:S(2)}, u32[]{:S(2)}) %collective-permute-start.10) | collective-permute-done | bytes 262176 | tf_op jit(solution)/shard_map/ppermute | solution.py:26
  247.0 4.1 %collective-permute-done.9 = f32[1,256,256]{2,1,0:T(8,128)S(1)} collective-permute-done((f32[1,256,256]{2,1,0:T(8,128)S(1)}, f32[1,256,256]{2,1,0:T(8,128)S(1)}, u32[]{:S(2)}, u32[]{:S(2)}) %collective-permute-start.9) | collective-permute-done | bytes 262176 | tf_op jit(solution)/shard_map/ppermute | solution.py:27
  251.2 2.0 fusion.10
  253.2 1.5 maximum_bitcast_fusion
  (173 shorter events, 21.9 us)
Async XLA Ops:
  6.5 8.2 %copy-start.4 = (f32[1,4,256,256]{3,2,1,0:T(8,128)S(1)}, f32[1,4,256,256]{3,2,1,0:T(8,128)}, u32[]{:S(2)}) copy-start(f32[1,4,256,256]{3,2,1,0:T(8,128)} %param.5) | copy-start | bytes 3145732
  6.5 1.7 copy-start.2
  6.5 2.5 copy-start
  6.5 58.2 %all-gather.2.cloned.1.call-start = ((), (), s32[]{:S(2)}) async-start(), calls=%async_computation | async-start | bytes 9437184 | tf_op jit(solution)/shard_map/all_gather | solution.py:16
  9.9 6.2 %collective-permute-start.3 = (f32[2,1,128,128]{3,2,1,0:T(8,128)S(1)}, f32[2,1,128,128]{3,2,1,0:T(8,128)S(1)}, u32[]{:S(2)}, u32[]{:S(2)}) collective-permute-start(f32[2,1,128,128]{3,2,1,0:T(8,128)S(1)} %get-tuple-element.197), channel_id=1, source_target_pairs={{0,1},{1,2},{2,3},{4,5},{5,6},{6,7},{8,9},{9,10},{10,11},{12,13},{... | collective-permute-start | bytes 393224 | tf_op jit(solution)/shard_map/ppermute | solution.py:26
  13.4 6.9 %collective-permute-start.4 = (f32[2,1,128,128]{3,2,1,0:T(8,128)S(1)}, f32[2,1,128,128]{3,2,1,0:T(8,128)S(1)}, u32[]{:S(2)}, u32[]{:S(2)}) collective-permute-start(f32[2,1,128,128]{3,2,1,0:T(8,128)S(1)} %get-tuple-element.198), channel_id=1, source_target_pairs={{1,0},{2,1},{3,2},{5,4},{6,5},{7,6},{9,8},{10,9},{11,10},{13,12},{... | collective-permute-start | bytes 393224 | tf_op jit(solution)/shard_map/ppermute | solution.py:27
  69.7 6.5 %collective-permute-start = (f32[2,128,128]{2,1,0:T(8,128)S(1)}, f32[2,128,128]{2,1,0:T(8,128)S(1)}, u32[]{:S(2)}, u32[]{:S(2)}) collective-permute-start(f32[2,128,128]{2,1,0:T(8,128)S(1)} %get-tuple-element.308), channel_id=1, source_target_pairs={{0,1},{1,2},{2,3},{4,5},{5,6},{6,7},{8,9},{9,10},{10,11},{12,13},{... | collective-permute-start | bytes 393224 | tf_op jit(solution)/shard_map/while/body/eval_jaxpr/ppermute | solution.py:26
  73.1 7.3 %collective-permute-start.1 = (f32[2,128,128]{2,1,0:T(8,128)S(1)}, f32[2,128,128]{2,1,0:T(8,128)S(1)}, u32[]{:S(2)}, u32[]{:S(2)}) collective-permute-start(f32[2,128,128]{2,1,0:T(8,128)S(1)} %get-tuple-element.308), channel_id=1, source_target_pairs={{1,0},{2,1},{3,2},{5,4},{6,5},{7,6},{9,8},{10,9},{11,10},{13,12},{... | collective-permute-start | bytes 393224 | tf_op jit(solution)/shard_map/while/body/eval_jaxpr/ppermute | solution.py:27
  81.5 6.3 %collective-permute-start.2 = (f32[2,128,128]{2,1,0:T(8,128)S(1)}, f32[2,128,128]{2,1,0:T(8,128)S(1)}, u32[]{:S(2)}, u32[]{:S(2)}) collective-permute-start(f32[2,128,128]{2,1,0:T(8,128)S(1)} %fusion.174), channel_id=1, source_target_pairs={{0,4},{4,8},{8,12},{12,16},{16,20},{20,24},{24,28},{1,5},{5,9},{9,... | collective-permute-start | bytes 393224 | tf_op jit(solution)/shard_map/while/body/eval_jaxpr/ppermute | solution.py:35
  87.9 5.9 %collective-permute-start = (f32[2,128,128]{2,1,0:T(8,128)S(1)}, f32[2,128,128]{2,1,0:T(8,128)S(1)}, u32[]{:S(2)}, u32[]{:S(2)}) collective-permute-start(f32[2,128,128]{2,1,0:T(8,128)S(1)} %get-tuple-element.308), channel_id=1, source_target_pairs={{0,1},{1,2},{2,3},{4,5},{5,6},{6,7},{8,9},{9,10},{10,11},{12,13},{... | collective-permute-start | bytes 393224 | tf_op jit(solution)/shard_map/while/body/eval_jaxpr/ppermute | solution.py:26
  91.3 6.9 %collective-permute-start.1 = (f32[2,128,128]{2,1,0:T(8,128)S(1)}, f32[2,128,128]{2,1,0:T(8,128)S(1)}, u32[]{:S(2)}, u32[]{:S(2)}) collective-permute-start(f32[2,128,128]{2,1,0:T(8,128)S(1)} %get-tuple-element.308), channel_id=1, source_target_pairs={{1,0},{2,1},{3,2},{5,4},{6,5},{7,6},{9,8},{10,9},{11,10},{13,12},{... | collective-permute-start | bytes 393224 | tf_op jit(solution)/shard_map/while/body/eval_jaxpr/ppermute | solution.py:27
  99.3 6.3 %collective-permute-start.2 = (f32[2,128,128]{2,1,0:T(8,128)S(1)}, f32[2,128,128]{2,1,0:T(8,128)S(1)}, u32[]{:S(2)}, u32[]{:S(2)}) collective-permute-start(f32[2,128,128]{2,1,0:T(8,128)S(1)} %fusion.174), channel_id=1, source_target_pairs={{0,4},{4,8},{8,12},{12,16},{16,20},{20,24},{24,28},{1,5},{5,9},{9,... | collective-permute-start | bytes 393224 | tf_op jit(solution)/shard_map/while/body/eval_jaxpr/ppermute | solution.py:35
  105.7 6.0 %collective-permute-start = (f32[2,128,128]{2,1,0:T(8,128)S(1)}, f32[2,128,128]{2,1,0:T(8,128)S(1)}, u32[]{:S(2)}, u32[]{:S(2)}) collective-permute-start(f32[2,128,128]{2,1,0:T(8,128)S(1)} %get-tuple-element.308), channel_id=1, source_target_pairs={{0,1},{1,2},{2,3},{4,5},{5,6},{6,7},{8,9},{9,10},{10,11},{12,13},{... | collective-permute-start | bytes 393224 | tf_op jit(solution)/shard_map/while/body/eval_jaxpr/ppermute | solution.py:26
  109.1 6.9 %collective-permute-start.1 = (f32[2,128,128]{2,1,0:T(8,128)S(1)}, f32[2,128,128]{2,1,0:T(8,128)S(1)}, u32[]{:S(2)}, u32[]{:S(2)}) collective-permute-start(f32[2,128,128]{2,1,0:T(8,128)S(1)} %get-tuple-element.308), channel_id=1, source_target_pairs={{1,0},{2,1},{3,2},{5,4},{6,5},{7,6},{9,8},{10,9},{11,10},{13,12},{... | collective-permute-start | bytes 393224 | tf_op jit(solution)/shard_map/while/body/eval_jaxpr/ppermute | solution.py:27
  117.1 6.3 %collective-permute-start.2 = (f32[2,128,128]{2,1,0:T(8,128)S(1)}, f32[2,128,128]{2,1,0:T(8,128)S(1)}, u32[]{:S(2)}, u32[]{:S(2)}) collective-permute-start(f32[2,128,128]{2,1,0:T(8,128)S(1)} %fusion.174), channel_id=1, source_target_pairs={{0,4},{4,8},{8,12},{12,16},{16,20},{20,24},{24,28},{1,5},{5,9},{9,... | collective-permute-start | bytes 393224 | tf_op jit(solution)/shard_map/while/body/eval_jaxpr/ppermute | solution.py:35
  123.5 5.4 %collective-permute-start = (f32[2,128,128]{2,1,0:T(8,128)S(1)}, f32[2,128,128]{2,1,0:T(8,128)S(1)}, u32[]{:S(2)}, u32[]{:S(2)}) collective-permute-start(f32[2,128,128]{2,1,0:T(8,128)S(1)} %get-tuple-element.308), channel_id=1, source_target_pairs={{0,1},{1,2},{2,3},{4,5},{5,6},{6,7},{8,9},{9,10},{10,11},{12,13},{... | collective-permute-start | bytes 393224 | tf_op jit(solution)/shard_map/while/body/eval_jaxpr/ppermute | solution.py:26
  125.5 7.5 %collective-permute-start.1 = (f32[2,128,128]{2,1,0:T(8,128)S(1)}, f32[2,128,128]{2,1,0:T(8,128)S(1)}, u32[]{:S(2)}, u32[]{:S(2)}) collective-permute-start(f32[2,128,128]{2,1,0:T(8,128)S(1)} %get-tuple-element.308), channel_id=1, source_target_pairs={{1,0},{2,1},{3,2},{5,4},{6,5},{7,6},{9,8},{10,9},{11,10},{13,12},{... | collective-permute-start | bytes 393224 | tf_op jit(solution)/shard_map/while/body/eval_jaxpr/ppermute | solution.py:27
  134.2 6.3 %collective-permute-start.2 = (f32[2,128,128]{2,1,0:T(8,128)S(1)}, f32[2,128,128]{2,1,0:T(8,128)S(1)}, u32[]{:S(2)}, u32[]{:S(2)}) collective-permute-start(f32[2,128,128]{2,1,0:T(8,128)S(1)} %fusion.174), channel_id=1, source_target_pairs={{0,4},{4,8},{8,12},{12,16},{16,20},{20,24},{24,28},{1,5},{5,9},{9,... | collective-permute-start | bytes 393224 | tf_op jit(solution)/shard_map/while/body/eval_jaxpr/ppermute | solution.py:35
  140.5 5.6 %collective-permute-start = (f32[2,128,128]{2,1,0:T(8,128)S(1)}, f32[2,128,128]{2,1,0:T(8,128)S(1)}, u32[]{:S(2)}, u32[]{:S(2)}) collective-permute-start(f32[2,128,128]{2,1,0:T(8,128)S(1)} %get-tuple-element.308), channel_id=1, source_target_pairs={{0,1},{1,2},{2,3},{4,5},{5,6},{6,7},{8,9},{9,10},{10,11},{12,13},{... | collective-permute-start | bytes 393224 | tf_op jit(solution)/shard_map/while/body/eval_jaxpr/ppermute | solution.py:26
  142.7 7.5 %collective-permute-start.1 = (f32[2,128,128]{2,1,0:T(8,128)S(1)}, f32[2,128,128]{2,1,0:T(8,128)S(1)}, u32[]{:S(2)}, u32[]{:S(2)}) collective-permute-start(f32[2,128,128]{2,1,0:T(8,128)S(1)} %get-tuple-element.308), channel_id=1, source_target_pairs={{1,0},{2,1},{3,2},{5,4},{6,5},{7,6},{9,8},{10,9},{11,10},{13,12},{... | collective-permute-start | bytes 393224 | tf_op jit(solution)/shard_map/while/body/eval_jaxpr/ppermute | solution.py:27
  151.4 6.3 %collective-permute-start.2 = (f32[2,128,128]{2,1,0:T(8,128)S(1)}, f32[2,128,128]{2,1,0:T(8,128)S(1)}, u32[]{:S(2)}, u32[]{:S(2)}) collective-permute-start(f32[2,128,128]{2,1,0:T(8,128)S(1)} %fusion.174), channel_id=1, source_target_pairs={{0,4},{4,8},{8,12},{12,16},{16,20},{20,24},{24,28},{1,5},{5,9},{9,... | collective-permute-start | bytes 393224 | tf_op jit(solution)/shard_map/while/body/eval_jaxpr/ppermute | solution.py:35
  157.7 5.6 %collective-permute-start = (f32[2,128,128]{2,1,0:T(8,128)S(1)}, f32[2,128,128]{2,1,0:T(8,128)S(1)}, u32[]{:S(2)}, u32[]{:S(2)}) collective-permute-start(f32[2,128,128]{2,1,0:T(8,128)S(1)} %get-tuple-element.308), channel_id=1, source_target_pairs={{0,1},{1,2},{2,3},{4,5},{5,6},{6,7},{8,9},{9,10},{10,11},{12,13},{... | collective-permute-start | bytes 393224 | tf_op jit(solution)/shard_map/while/body/eval_jaxpr/ppermute | solution.py:26
  159.9 7.5 %collective-permute-start.1 = (f32[2,128,128]{2,1,0:T(8,128)S(1)}, f32[2,128,128]{2,1,0:T(8,128)S(1)}, u32[]{:S(2)}, u32[]{:S(2)}) collective-permute-start(f32[2,128,128]{2,1,0:T(8,128)S(1)} %get-tuple-element.308), channel_id=1, source_target_pairs={{1,0},{2,1},{3,2},{5,4},{6,5},{7,6},{9,8},{10,9},{11,10},{13,12},{... | collective-permute-start | bytes 393224 | tf_op jit(solution)/shard_map/while/body/eval_jaxpr/ppermute | solution.py:27
  168.6 6.3 %collective-permute-start.2 = (f32[2,128,128]{2,1,0:T(8,128)S(1)}, f32[2,128,128]{2,1,0:T(8,128)S(1)}, u32[]{:S(2)}, u32[]{:S(2)}) collective-permute-start(f32[2,128,128]{2,1,0:T(8,128)S(1)} %fusion.174), channel_id=1, source_target_pairs={{0,4},{4,8},{8,12},{12,16},{16,20},{20,24},{24,28},{1,5},{5,9},{9,... | collective-permute-start | bytes 393224 | tf_op jit(solution)/shard_map/while/body/eval_jaxpr/ppermute | solution.py:35
  175.0 5.6 %collective-permute-start = (f32[2,128,128]{2,1,0:T(8,128)S(1)}, f32[2,128,128]{2,1,0:T(8,128)S(1)}, u32[]{:S(2)}, u32[]{:S(2)}) collective-permute-start(f32[2,128,128]{2,1,0:T(8,128)S(1)} %get-tuple-element.308), channel_id=1, source_target_pairs={{0,1},{1,2},{2,3},{4,5},{5,6},{6,7},{8,9},{9,10},{10,11},{12,13},{... | collective-permute-start | bytes 393224 | tf_op jit(solution)/shard_map/while/body/eval_jaxpr/ppermute | solution.py:26
  177.2 7.5 %collective-permute-start.1 = (f32[2,128,128]{2,1,0:T(8,128)S(1)}, f32[2,128,128]{2,1,0:T(8,128)S(1)}, u32[]{:S(2)}, u32[]{:S(2)}) collective-permute-start(f32[2,128,128]{2,1,0:T(8,128)S(1)} %get-tuple-element.308), channel_id=1, source_target_pairs={{1,0},{2,1},{3,2},{5,4},{6,5},{7,6},{9,8},{10,9},{11,10},{13,12},{... | collective-permute-start | bytes 393224 | tf_op jit(solution)/shard_map/while/body/eval_jaxpr/ppermute | solution.py:27
  185.9 6.3 %collective-permute-start.2 = (f32[2,128,128]{2,1,0:T(8,128)S(1)}, f32[2,128,128]{2,1,0:T(8,128)S(1)}, u32[]{:S(2)}, u32[]{:S(2)}) collective-permute-start(f32[2,128,128]{2,1,0:T(8,128)S(1)} %fusion.174), channel_id=1, source_target_pairs={{0,4},{4,8},{8,12},{12,16},{16,20},{20,24},{24,28},{1,5},{5,9},{9,... | collective-permute-start | bytes 393224 | tf_op jit(solution)/shard_map/while/body/eval_jaxpr/ppermute | solution.py:35
  192.5 9.3 %collective-permute-start.6 = (f32[2,128,128]{2,1,0:T(8,128)S(1)}, f32[2,128,128]{2,1,0:T(8,128)S(1)}, u32[]{:S(2)}, u32[]{:S(2)}) collective-permute-start(f32[2,128,128]{2,1,0:T(8,128)S(1)} %get-tuple-element.121), channel_id=1, source_target_pairs={{1,0},{2,1},{3,2},{5,4},{6,5},{7,6},{9,8},{10,9},{11,10},{13,12},{... | collective-permute-start | bytes 393224 | tf_op jit(solution)/shard_map/ppermute | solution.py:27
  193.8 7.9 %collective-permute-start.5 = (f32[2,128,128]{2,1,0:T(8,128)S(1)}, f32[2,128,128]{2,1,0:T(8,128)S(1)}, u32[]{:S(2)}, u32[]{:S(2)}) collective-permute-start(f32[2,128,128]{2,1,0:T(8,128)S(1)} %get-tuple-element.121), channel_id=1, source_target_pairs={{0,1},{1,2},{2,3},{4,5},{5,6},{6,7},{8,9},{9,10},{10,11},{12,13},{... | collective-permute-start | bytes 393224 | tf_op jit(solution)/shard_map/ppermute | solution.py:26
  204.1 1.2 copy-start.5
  206.7 20.9 %collective-permute-start.8 = (f32[3,1,256,256]{3,2,1,0:T(8,128)S(1)}, f32[3,1,256,256]{3,2,1,0:T(8,128)S(1)}, u32[]{:S(2)}, u32[]{:S(2)}) collective-permute-start(f32[3,1,256,256]{3,2,1,0:T(8,128)S(1)} %get-tuple-element.159), channel_id=1, source_target_pairs={{0,1},{1,2},{2,3},{4,5},{5,6},{6,7},{8,9},{9,10},{10,11},{12,13},{... | collective-permute-start | bytes 2359304 | tf_op jit(solution)/shard_map/ppermute | solution.py:26
  211.1 20.7 %collective-permute-start.7 = (f32[3,1,256,256]{3,2,1,0:T(8,128)S(1)}, f32[3,1,256,256]{3,2,1,0:T(8,128)S(1)}, u32[]{:S(2)}, u32[]{:S(2)}) collective-permute-start(f32[3,1,256,256]{3,2,1,0:T(8,128)S(1)} %get-tuple-element.160), channel_id=1, source_target_pairs={{1,0},{2,1},{3,2},{5,4},{6,5},{7,6},{9,8},{10,9},{11,10},{13,12},{... | collective-permute-start | bytes 2359304 | tf_op jit(solution)/shard_map/ppermute | solution.py:27
  227.6 4.2 %copy-start.6 = (f32[3,1,256,256]{3,2,1,0:T(8,128)}, f32[3,1,256,256]{3,2,1,0:T(8,128)S(1)}, u32[]{:S(2)}) copy-start(f32[3,1,256,256]{3,2,1,0:T(8,128)S(1)} %collective-permute-done.8) | copy-start | bytes 2359300
  231.8 0.9 copy-start.7
  240.2 11.0 %copy-start.1 = (f32[4,256,256]{2,1,0:T(8,128)S(1)}, f32[4,256,256]{2,1,0:T(8,128)}, u32[]{:S(2)}) copy-start(f32[4,256,256]{2,1,0:T(8,128)} %param.7) | copy-start | bytes 3145732
  240.2 11.0 %copy-start.3 = (f32[1,4,256,256]{3,2,1,0:T(8,128)S(1)}, f32[1,4,256,256]{3,2,1,0:T(8,128)}, u32[]{:S(2)}) copy-start(f32[1,4,256,256]{3,2,1,0:T(8,128)} %param.6) | copy-start | bytes 3145732
  240.6 6.5 %collective-permute-start.10 = (f32[1,256,256]{2,1,0:T(8,128)S(1)}, f32[1,256,256]{2,1,0:T(8,128)S(1)}, u32[]{:S(2)}, u32[]{:S(2)}) collective-permute-start(f32[1,256,256]{2,1,0:T(8,128)S(1)} %get-tuple-element.169), channel_id=1, source_target_pairs={{0,1},{1,2},{2,3},{4,5},{5,6},{6,7},{8,9},{9,10},{10,11},{12,13},{... | collective-permute-start | bytes 786440 | tf_op jit(solution)/shard_map/ppermute | solution.py:26
  242.9 8.3 %collective-permute-start.9 = (f32[1,256,256]{2,1,0:T(8,128)S(1)}, f32[1,256,256]{2,1,0:T(8,128)S(1)}, u32[]{:S(2)}, u32[]{:S(2)}) collective-permute-start(f32[1,256,256]{2,1,0:T(8,128)S(1)} %get-tuple-element.170), channel_id=1, source_target_pairs={{1,0},{2,1},{3,2},{5,4},{6,5},{7,6},{9,8},{10,9},{11,10},{13,12},{... | collective-permute-start | bytes 786440 | tf_op jit(solution)/shard_map/ppermute | solution.py:27
Sparse Core Ops, SparseCore 0:
  9.2 55.4 all-gather.1
